TPU v7x, 32 devices: a whole 2x2x4 slice. The times are simulated.
32 devices in a mesh: gossip: 16 (over z, y, core), mp: 2 (over x).
Axes of the slice: x: 2, y: 2, z: 4, core: 2. Of those that a mesh axis runs over, the one named last changes fastest.
Arguments:
- params: float32 [16, 1024, 4096], P('gossip', None, 'mp'), may hold values from -6 to 6
- public: float32 [16, 1024, 64], P('gossip'), may hold values from -12 to 12
- gradients: bfloat16 [2, 16, 1024, 4096], P(None, 'gossip', None, 'mp'), may hold values from -130 to 130
- projection: float32 [4096, 64], P('mp'), may hold values from -0.09375 to 0.09375
- partners: int32 [2, 16], P(None, 'gossip'), may hold values from 0 to 15, as said below
Outputs:
- params_out: float32 [16, 1024, 4096], P('gossip', None, 'mp')
- public_out: float32 [16, 1024, 64], P('gossip')
- consensus: float32 [2], replicated
- grad_norm: float32 [2], replicated
Inputs may be any that keep to these rules, and one draw needn't show every extreme that they name: Each row is a pairing of the 16 replicas: partners[r, partners[r, i]] = i and partners[r, i] != i.
All inputs are finite; a program needn't handle non-finite values.
Results may differ from a plain program's by a relative error of at most 0.008.
Values may be sent and summed in bfloat16 or wider, within the bound.
A program may use at most 64 MiB of HBM per device.

v0:
```python
import jax
import jax.numpy as jnp
from jax import lax
from jax.sharding import PartitionSpec as P

ROUNDS = 2


step_size = 1.0
clip_limit = 0.5
mixing = 0.4
epsilon = 1e-06


def partner_rows(outgoing, table_row):
    initial = outgoing.shape
    entries = outgoing.size
    replicas = lax.axis_size("gossip")
    pieces = outgoing.reshape(replicas, entries // replicas)
    spread = lax.all_to_all(pieces, "gossip", split_axis=0, concat_axis=0, tiled=True)
    reordered = jnp.take(spread, table_row, axis=0)
    back = lax.all_to_all(reordered, "gossip", split_axis=0, concat_axis=0, tiled=True)
    return back.reshape(initial)


def body(params, public, gradients, projection, partners):
    highest = lax.Precision.HIGHEST
    mp_count = lax.axis_size("mp")
    row_count = params.shape[1]
    total = lax.axis_size("gossip") * row_count * projection.shape[0] * mp_count
    weights = params[0]
    public_state = public[0]
    drift_list = []
    norm_list = []
    whole_table = lax.all_gather(partners, "gossip", axis=1, tiled=True)
    for round_index in range(ROUNDS):
        grad_local = gradients[round_index, 0].astype(jnp.float32)
        local_squares = jnp.sum(grad_local * grad_local)
        squares = lax.psum(local_squares, ("gossip", "mp"))
        norm_value = jnp.sqrt(squares / total + epsilon)
        norm_list.append(norm_value)
        scale = jnp.minimum(1.0, clip_limit / norm_value)
        half = weights - step_size * scale * grad_local
        table_row = whole_table[round_index]
        coef_rows = public_state
        rebuilt = jnp.dot(coef_rows, projection.T, precision=highest)
        summed = lax.psum(jnp.dot(half - rebuilt, projection, precision=highest), "mp")
        sent = (public_state + summed).astype(jnp.bfloat16)
        mate = partner_rows(sent, table_row)
        public_state = sent.astype(jnp.float32)
        drift = jnp.dot(mate.astype(jnp.float32) - public_state, projection.T, precision=highest)
        weights = half + mixing * drift
        local_drift = jnp.sum(drift * drift)
        drift_list.append(lax.psum(local_drift, ("gossip", "mp")) / total)
    return (weights[None], public_state[None], jnp.stack(drift_list), jnp.stack(norm_list))


def solution(mesh):
    return jax.shard_map(
        body,
        mesh=mesh,
        in_specs=(
            P("gossip", None, "mp"),
            P("gossip", None, None),
            P(None, "gossip", None, "mp"),
            P("mp", None),
            P(None, "gossip"),
        ),
        out_specs=(P("gossip", None, "mp"), P("gossip", None, None), P(), P()),
        check_vma=False,
    )
```

profile of v0, /device:TPU:12, one launch (start us, length us, event | category | flops | bytes accessed | tf_op | source)
XLA Modules:
  0.0 274.4 jit_solution(1007616994653139488)
XLA Ops:
  7.2 0.0 copy-start
  7.2 0.0 copy-start.2
  7.2 0.0 all-reduce.5.cloned.1.call-start
  7.2 5.2 %fusion.3 = (f32[]{:T(128)}, f32[]{:T(128)}) fusion(bf16[2,1,1024,2048]{3,2,1,0:T(8,128)(2,1)} %param.9), kind=kLoop, calls=%fused_computation.9 | loop fusion | flops 12582910 | bytes 8388616 | tf_op jit(solution)/shard_map/reduce_sum | solution.py:38
  12.4 41.6 %all-reduce.1 = (f32[]{:T(128)}, f32[]{:T(128)}) all-reduce(f32[]{:T(128)} %get-tuple-element.6, f32[]{:T(128)} %get-tuple-element.5), channel_id=1, replica_groups=mesh['gossip'=16,'mp'=2] {'gossip','mp'}, use_global_device_ids=true, to_apply=%region_1.0 | all-reduce | flops 2 | bytes 16 | tf_op jit(solution)/shard_map/psum | solution.py:39
  54.8 0.0 copy-done
  54.8 0.0 copy-done.2
  54.8 6.7 %fusion.16 = f32[1024,2048]{1,0:T(8,128)S(1)} fusion(f32[2048,64]{0,1:T(8,128)S(1)} %copy-done, f32[1,1024,64]{1,2,0:T(8,128)S(1)} %copy-done.2), kind=kOutput, calls=%fused_computation.29 | convolution fusion | flops 1610612736 | bytes 9175040 | tf_op jit(solution)/shard_map/dot_general | solution.py:46
  61.5 0.0 copy-start.3
  61.6 12.9 %fusion.8 = f32[1024,64]{0,1:T(8,128)} fusion(f32[2048,64]{0,1:T(8,128)S(1)} %copy-done, f32[1024,2048]{1,0:T(8,128)S(1)} %fusion.16, f32[1,1024,2048]{2,1,0:T(8,128)} %param.7, f32[]{:T(128)S(6)} %min.6, bf16[2,1,1024,2048]{3,2,1,0:T(8,128)(2,1)} %param.9), kind=kOutput, calls=%fused_computation.17 | convolution fusion | flops 1619001344 | bytes 21757956 | tf_op jit(solution)/shard_map/dot_general | solution.py:47
  74.4 0.0 all-reduce.5.cloned.1.call-update
  75.2 14.1 %all-gather = s32[16,1,2]{2,1,0:T(1,128)S(1)} all-gather(s32[1,1,2]{2,1,0:T(1,128)S(1)} %bitcast.64), channel_id=1, replica_groups=mesh['gossip'=16,'mp'=2] {'gossip'}, dimensions={0}, use_global_device_ids=true | all-gather | bytes 136 | tf_op jit(solution)/shard_map/all_gather | solution.py:35
  89.3 0.1 copy.24
  89.4 7.5 %all-reduce.5.cloned.1.call-done = f32[1024,64]{0,1:T(8,128)} async-done(((f32[1024,64]{0,1:T(8,128)}), f32[1024,64]{0,1:T(8,128)}) %all-reduce.5.cloned.1.call-update) | async-done | bytes 262160 | tf_op jit(solution)/shard_map/psum | solution.py:47
  96.9 1.0 fusion.18
  97.9 0.2 copy.25
  98.0 0.2 all_to_all.38
  98.2 0.5 broadcast.54
  98.7 1.4 reduce.6
  100.1 0.7 reshape.71
  100.8 6.1 %all-to-all-start = ((bf16[16,2,2048]{2,1,0:T(2,128)(2,1)}), bf16[16,2,2048]{2,1,0:T(2,128)(2,1)S(1)}, u32[]{:S(2)}, u32[]{:S(2)}) async-start(bf16[16,2,2048]{2,1,0:T(2,128)(2,1)} %reshape.71), calls=%async_computation | async-start | bytes 262144 | tf_op jit(solution)/shard_map/all_to_all | solution.py:20
  106.9 4.8 %all-to-all-done = bf16[16,2,2048]{2,1,0:T(2,128)(2,1)S(1)} async-done(((bf16[16,2,2048]{2,1,0:T(2,128)(2,1)}), bf16[16,2,2048]{2,1,0:T(2,128)(2,1)S(1)}, u32[]{:S(2)}, u32[]{:S(2)}) %all-to-all-start) | async-done | bytes 131104 | tf_op jit(solution)/shard_map/all_to_all | solution.py:20
  111.7 0.1 reshape.72
  111.8 0.2 copy.38
  112.0 0.6 gather_fusion
  112.6 0.1 select_bitcast_fusion.1
  112.7 0.7 reduce.7
  113.4 0.7 reshape.73
  114.1 6.5 %all-to-all-start.1 = ((bf16[16,2,2048]{2,1,0:T(2,128)(2,1)}), bf16[16,2,2048]{2,1,0:T(2,128)(2,1)S(1)}, u32[]{:S(2)}, u32[]{:S(2)}) async-start(bf16[16,2,2048]{2,1,0:T(2,128)(2,1)} %reshape.73), calls=%async_computation.1 | async-start | bytes 262144 | tf_op jit(solution)/shard_map/all_to_all | solution.py:22
  120.6 0.0 all-reduce.7.cloned.1.call-start
  120.7 5.7 %fusion.20 = f32[1024,2048]{1,0:T(8,128)} fusion(bf16[1024,64]{0,1:T(8,128)(2,1)S(1)} %fusion.18, f32[2048,64]{0,1:T(8,128)S(1)} %copy-done), kind=kOutput, calls=%fused_computation.46 | convolution fusion | flops 1610612736 | bytes 9043968 | tf_op jit(solution)/shard_map/dot_general | solution.py:46
  126.3 0.0 all-to-all-done.1
  126.3 0.1 reshape.74
  126.5 0.7 convert_reduce_fusion.1
  127.2 0.2 reshape.41
  127.4 0.2 copy.28
  127.6 14.2 %multiply_reduce_fusion.1 = (f32[]{:T(128)}, f32[1024,2048]{1,0:T(8,128)S(1)}) fusion(bf16[2,1,1024,2048]{3,2,1,0:T(8,128)(2,1)} %param.9, f32[]{:T(128)S(6)} %min.7, f32[]{:T(128)S(6)} %min.6, f32[1,1024,2048]{2,1,0:T(8,128)} %param.7, f32[2048,64]{0,1:T(8,128)S(1)} %copy-done, f32[1024,64]{0,1:T(8,128)S(1)} %copy.28, bf16[1024,64]{0,1:T(8,128)(2,1)S(1)} %fusion.18), kind=kOutput, calls=%fused_computation.13 | convolution fusion | flops 1631715328 | bytes 26083340 | tf_op jit(solution)/shard_map/dot_general | solution.py:51
  141.9 3.4 %copy-done.1 = f32[1024,2048]{1,0:T(8,128)} copy-done((f32[1024,2048]{1,0:T(8,128)}, f32[1024,2048]{1,0:T(8,128)S(1)}, u32[]{:S(2)}) %copy-start.1) | copy-done | bytes 8388632
  145.2 11.4 %fusion.6 = f32[1024,64]{0,1:T(8,128)} fusion(f32[2048,64]{0,1:T(8,128)S(1)} %copy-done, f32[1024,2048]{1,0:T(8,128)S(1)} %get-tuple-element.18, f32[1024,2048]{1,0:T(8,128)} %fusion.20), kind=kOutput, calls=%fused_computation.15 | convolution fusion | flops 1612709888 | bytes 17563648 | tf_op jit(solution)/shard_map/dot_general | solution.py:47
  156.7 0.0 all-reduce.7.cloned.1.call-update
  156.7 23.5 %all-reduce.7.cloned.1.call-done = f32[1024,64]{0,1:T(8,128)} async-done(((f32[1024,64]{0,1:T(8,128)}), f32[1024,64]{0,1:T(8,128)}) %all-reduce.7.cloned.1.call-update) | async-done | bytes 262160 | tf_op jit(solution)/shard_map/psum | solution.py:47
  180.2 1.7 convert_bitcast_fusion
  181.8 0.2 copy.29
  182.0 0.2 all_to_all.39
  182.2 1.4 reduce.8
  183.6 0.7 reshape.75
  184.3 6.1 %all-to-all-start.2 = ((bf16[16,2,2048]{2,1,0:T(2,128)(2,1)}), bf16[16,2,2048]{2,1,0:T(2,128)(2,1)S(1)}, u32[]{:S(2)}, u32[]{:S(2)}) async-start(bf16[16,2,2048]{2,1,0:T(2,128)(2,1)} %reshape.75), calls=%async_computation.2 | async-start | bytes 262144 | tf_op jit(solution)/shard_map/all_to_all | solution.py:20
  190.3 4.8 %all-to-all-done.2 = bf16[16,2,2048]{2,1,0:T(2,128)(2,1)S(1)} async-done(((bf16[16,2,2048]{2,1,0:T(2,128)(2,1)}), bf16[16,2,2048]{2,1,0:T(2,128)(2,1)S(1)}, u32[]{:S(2)}, u32[]{:S(2)}) %all-to-all-start.2) | async-done | bytes 131104 | tf_op jit(solution)/shard_map/all_to_all | solution.py:20
  195.1 0.1 reshape.76
  195.3 0.2 copy.37
  195.4 0.6 gather_fusion.1
  196.1 0.1 select_bitcast_fusion
  196.1 0.7 reduce.9
  196.8 0.7 reshape.77
  197.5 6.5 %all-to-all-start.3 = ((bf16[16,2,2048]{2,1,0:T(2,128)(2,1)}), bf16[16,2,2048]{2,1,0:T(2,128)(2,1)S(1)}, u32[]{:S(2)}, u32[]{:S(2)}) async-start(bf16[16,2,2048]{2,1,0:T(2,128)(2,1)} %reshape.77), calls=%async_computation.3 | async-start | bytes 262144 | tf_op jit(solution)/shard_map/all_to_all | solution.py:22
  204.1 0.6 pad_maximum_fusion.1
  204.6 4.3 %all-to-all-done.3 = bf16[16,2,2048]{2,1,0:T(2,128)(2,1)S(1)} async-done(((bf16[16,2,2048]{2,1,0:T(2,128)(2,1)}), bf16[16,2,2048]{2,1,0:T(2,128)(2,1)S(1)}, u32[]{:S(2)}, u32[]{:S(2)}) %all-to-all-start.3) | async-done | bytes 131104 | tf_op jit(solution)/shard_map/all_to_all | solution.py:22
  208.9 0.1 reshape.78
  209.0 0.7 convert_reduce_fusion
  209.8 0.2 reshape.42
  210.0 0.2 copy.32
  210.2 13.3 %multiply_reduce_fusion = (f32[]{:T(128)}, f32[1,1024,2048]{2,1,0:T(8,128)}) fusion(f32[1024,2048]{1,0:T(8,128)} %copy-done.1, f32[2048,64]{0,1:T(8,128)S(1)} %copy-done, f32[1024,64]{0,1:T(8,128)S(1)} %copy.32, bf16[1024,64]{0,1:T(8,128)(2,1)S(1)} %get-tuple-element.12), kind=kOutput, calls=%fused_computation.12 | convolution fusion | flops 1619132416 | bytes 17694724 | tf_op jit(solution)/shard_map/dot_general | solution.py:51
  223.5 42.2 %all-reduce = (f32[]{:T(128)}, f32[]{:T(128)}) all-reduce(f32[]{:T(128)} %get-tuple-element.19, f32[]{:T(128)} %get-tuple-element.17), channel_id=1, replica_groups=mesh['gossip'=16,'mp'=2] {'gossip','mp'}, use_global_device_ids=true, to_apply=%region_9.11 | all-reduce | flops 2 | bytes 16 | tf_op jit(solution)/shard_map/psum | solution.py:54
  267.0 0.6 pad_maximum_fusion
  (5 shorter events, 0.0 us)
Async XLA Ops:
  7.2 47.6 %copy-start = (f32[2048,64]{0,1:T(8,128)S(1)}, f32[2048,64]{0,1:T(8,128)}, u32[]{:S(2)}) copy-start(f32[2048,64]{0,1:T(8,128)} %param.10) | copy-start | bytes 1572868
  7.2 47.6 %copy-start.2 = (f32[1,1024,64]{1,2,0:T(8,128)S(1)}, f32[1,1024,64]{1,2,0:T(8,128)}, u32[]{:S(2)}) copy-start(f32[1,1024,64]{1,2,0:T(8,128)} %param.8) | copy-start | bytes 786436
  7.2 89.7 %all-reduce.5.cloned.1.call-start = ((), (), s32[]{:S(2)}) async-start(), calls=%async_computation.4 | async-start | bytes 524288 | tf_op jit(solution)/shard_map/psum | solution.py:47
  61.5 13.6 %copy-start.3 = (s32[2,1]{0,1:T(1,128)S(1)}, s32[2,1]{0,1:T(1,128)}, u32[]{:S(2)}) copy-start(s32[2,1]{0,1:T(1,128)} %param.11) | copy-start | bytes 28
  100.8 10.9 %all-to-all-start = ((bf16[16,2,2048]{2,1,0:T(2,128)(2,1)}), bf16[16,2,2048]{2,1,0:T(2,128)(2,1)S(1)}, u32[]{:S(2)}, u32[]{:S(2)}) async-start(bf16[16,2,2048]{2,1,0:T(2,128)(2,1)} %reshape.71), calls=%async_computation | async-start | bytes 262144 | tf_op jit(solution)/shard_map/all_to_all | solution.py:20
  114.1 12.2 %all-to-all-start.1 = ((bf16[16,2,2048]{2,1,0:T(2,128)(2,1)}), bf16[16,2,2048]{2,1,0:T(2,128)(2,1)S(1)}, u32[]{:S(2)}, u32[]{:S(2)}) async-start(bf16[16,2,2048]{2,1,0:T(2,128)(2,1)} %reshape.73), calls=%async_computation.1 | async-start | bytes 262144 | tf_op jit(solution)/shard_map/all_to_all | solution.py:22
  120.6 59.5 %all-reduce.7.cloned.1.call-start = ((), (), s32[]{:S(2)}) async-start(), calls=%async_computation.5 | async-start | bytes 524288 | tf_op jit(solution)/shard_map/psum | solution.py:47
  141.9 3.4 %copy-start.1 = (f32[1024,2048]{1,0:T(8,128)}, f32[1024,2048]{1,0:T(8,128)S(1)}, u32[]{:S(2)}) copy-start(f32[1024,2048]{1,0:T(8,128)S(1)} %get-tuple-element.18) | copy-start | bytes 25165828
  184.3 10.9 %all-to-all-start.2 = ((bf16[16,2,2048]{2,1,0:T(2,128)(2,1)}), bf16[16,2,2048]{2,1,0:T(2,128)(2,1)S(1)}, u32[]{:S(2)}, u32[]{:S(2)}) async-start(bf16[16,2,2048]{2,1,0:T(2,128)(2,1)} %reshape.75), calls=%async_computation.2 | async-start | bytes 262144 | tf_op jit(solution)/shard_map/all_to_all | solution.py:20
  197.5 11.4 %all-to-all-start.3 = ((bf16[16,2,2048]{2,1,0:T(2,128)(2,1)}), bf16[16,2,2048]{2,1,0:T(2,128)(2,1)S(1)}, u32[]{:S(2)}, u32[]{:S(2)}) async-start(bf16[16,2,2048]{2,1,0:T(2,128)(2,1)} %reshape.77), calls=%async_computation.3 | async-start | bytes 262144 | tf_op jit(solution)/shard_map/all_to_all | solution.py:22
Sparse Core Ops, SparseCore 0:
  74.6 22.2 all-reduce.4
  156.8 23.2 all-reduce.6
where the time goes:
time: 275 us; the launch traced here: 274 us
  blocking collectives  97.9 us (36%)
  matrix products  64.2 us (23%)
  waiting for transfers between devices  44.8 us (16%)
  starting transfers between devices  25.2 us (9%)
  between operations  17.1 us (6%)
  other arithmetic  14.8 us (5%)
  local copies, waits for them, and re-layouts  10.4 us (4%)
    psum x1, blocking collectives, body(): drift_list.append(lax.psum(local_drift, ('gossip', 'mp')) / total)  42.2 us
    psum x1, blocking collectives, body(): squares = lax.psum(local_squares, ('gossip', 'mp'))  41.6 us
    psum x2, waiting for transfers between devices, body(): lax.psum(jnp.dot(half - rebuilt, projection, precision=highest), 'mp')  31 us
    dot_general x2, matrix products, body(): jnp.dot(mate.astype(jnp.float32) - public_state, projection.T, precision=...  27.6 us
    dot_general x2, matrix products, body(): jnp.dot(half - rebuilt, projection, precision=highest)  24.3 us
    all_gather x1, blocking collectives, body(): whole_table = lax.all_gather(partners, 'gossip', axis=1, tiled=True)  14.1 us
    all_to_all x2, starting transfers between devices, partner_rows(): lax.all_to_all(reordered, 'gossip', split_axis=0, concat_axis=0, tiled=True)  13 us
    dot_general x2, matrix products, body(): rebuilt = jnp.dot(coef_rows, projection.T, precision=highest)  12.4 us
  transfers between devices with their start and end apart: 6, of which 5 were waited for; matrix products, arithmetic and copies ran while one was open for 2% of the time, Pallas kernels for 0%

commit v1 on v0

v1 whole, which is shorter than its diff:
```python
import functools

import jax
import jax.numpy as jnp
from jax import lax
from jax.experimental import pallas as pl
from jax.experimental.pallas import tpu as pltpu
from jax.sharding import PartitionSpec as P

ROUNDS = 2
step_size = 1.0
clip_limit = 0.5
mixing = 0.4
epsilon = 1e-06

F32 = jnp.float32
BF16 = jnp.bfloat16
HIGHEST = lax.Precision.HIGHEST
VMEM = pl.BlockSpec(memory_space=pltpu.VMEM)
SMEM = pl.BlockSpec(memory_space=pltpu.SMEM)


def high_low(value):
    high = value.astype(BF16)
    return high, (value - high.astype(F32)).astype(BF16)


def dot(a, b):
    return jnp.dot(a, b, preferred_element_type=F32)


def project(mp, w_ref, g_ref, c_ref, p_ref, a_ref, b_ref, d_ref, gram_ref, sq_ref, basis, mixer):
    rank = p_ref.shape[1]
    tile, columns = w_ref.shape[1:]

    @pl.when(pl.program_id(0) == 0)
    def _():
        high, low = high_low(p_ref[...])
        basis[...] = jnp.concatenate([high, low], axis=1)
        parts = lax.dot_general(basis[...], basis[...], (((0,), (0,)), ((), ())), preferred_element_type=F32)
        folded = parts + pltpu.roll(parts, rank, 1)
        gram = folded[:rank] + folded[rank:]
        row = lax.broadcasted_iota(jnp.int32, gram.shape, 0)
        col = lax.broadcasted_iota(jnp.int32, gram.shape, 1)
        gram = jnp.where(col < rank, gram, 0.0)
        gram_ref[...] = gram
        mixer[...] = jnp.where(row == col, 1.0 / mp, 0.0) - gram
        sq_ref[...] = jnp.zeros_like(sq_ref)

    def fold(value):
        return value + pltpu.roll(value, rank, 1)

    for index in range(ROUNDS):
        grad = g_ref[index, 0]
        wide = grad.astype(F32)
        sq_ref[index] += jnp.sum((wide * wide).reshape(tile // 8, 8, columns), axis=0)
        product = fold(dot(grad, basis[...]))
        if index == 0:
            b_ref[...] = product
        else:
            lane = lax.broadcasted_iota(jnp.int32, product.shape, 1)
            d_ref[...] = jnp.where(lane < rank, 0.0, product)
    high, low = high_low(w_ref[0])
    product = fold(dot(high, basis[...]) + dot(low, basis[...]))
    a_ref[...] = product + jnp.dot(c_ref[0], mixer[...], precision=HIGHEST, preferred_element_type=F32)


def exchange(groups, members, total, a_ref, b_ref, d_ref, gram_ref, sq_ref, partners_ref, f_ref, stat_ref,
             tiles, tiles_mp, grams, local, arrived, owned, first, reply, second, final, cons, cons_mp,
             send_g, recv_g, send_m, recv_m):
    g = lax.axis_index("gossip")
    m = lax.axis_index("mp")
    rows = owned.shape[1]
    lanes = owned.shape[2]
    rank = lanes // 2
    flat = groups * rows

    def peers(count, here, act):
        lax.fori_loop(1, count, lambda k, _: (act(lax.rem(here + k, count)), 0)[1], 0)

    barrier = pltpu.get_barrier_semaphore()

    def greet(axis):
        def act(peer):
            pl.semaphore_signal(barrier, inc=1, device_id={axis: peer}, device_id_type=pl.DeviceIdType.MESH)
        return act

    peers(groups, g, greet("gossip"))
    peers(members, m, greet("mp"))

    def copy(axis, slot, src, dst, peer, into):
        send, recv = (send_g, recv_g) if axis == "gossip" else (send_m, recv_m)
        return pltpu.make_async_remote_copy(
            src_ref=src, dst_ref=dst, send_sem=send.at[slot, peer], recv_sem=recv.at[slot, into],
            device_id={axis: peer}, device_id_type=pl.DeviceIdType.MESH)

    def start(axis, slot, source, target):
        count, here = (groups, g) if axis == "gossip" else (members, m)
        peers(count, here, lambda p: copy(axis, slot, source(p), target.at[here], p, here).start())

    def finish(axis, slot, source, target):
        count, here = (groups, g) if axis == "gossip" else (members, m)
        peers(count, here, lambda p: copy(axis, slot, source(p), target.at[p], p, p).wait())

    row = lax.broadcasted_iota(jnp.int32, (8, 128), 0)
    tile = jnp.where(row == 0, jnp.sum(sq_ref[0]), jnp.sum(sq_ref[1]))
    tile = jnp.where(row == 2, partners_ref[0, 0].astype(F32), tile)
    tile = jnp.where(row == 3, partners_ref[1, 0].astype(F32), tile)
    tiles[g] = tile
    grams[m] = gram_ref[...]
    pl.semaphore_wait(barrier, groups - 1 + members - 1)

    start("gossip", 0, lambda p: tiles.at[g], tiles)
    start("mp", 0, lambda p: grams.at[m], grams)
    finish("gossip", 0, lambda p: tiles.at[g], tiles)
    tiles_mp[m] = jnp.sum(tiles[...], axis=0)
    start("mp", 1, lambda p: tiles_mp.at[m], tiles_mp)
    finish("mp", 1, lambda p: tiles_mp.at[m], tiles_mp)
    norm = jnp.sqrt(jnp.sum(tiles_mp[...], axis=0) / total + epsilon)
    scale = step_size * jnp.minimum(1.0, clip_limit / norm)

    local[...] = a_ref[...] - scale[0:1, :] * b_ref[...] - scale[1:2, :] * d_ref[...]
    start("mp", 2, lambda p: local.at[p], arrived)
    summed = local[m]
    finish("mp", 2, lambda p: local.at[p], arrived)
    arrived[m] = summed
    summed = arrived[0]
    for index in range(1, members):
        summed = summed + arrived[index]
    lane = lax.broadcasted_iota(jnp.int32, summed.shape, 2)
    owned[...] = jnp.where(lane < rank, summed.astype(BF16).astype(F32), summed)
    start("gossip", 1, lambda p: owned.at[p], first)
    first[g] = owned[g]

    finish("mp", 0, lambda p: grams.at[m], grams)
    gram = jnp.sum(grams[...], axis=0)[:, :rank]
    inside = lax.broadcasted_iota(jnp.int32, (rows, flat), 0).astype(F32)
    column = lax.broadcasted_iota(jnp.int32, (rows, flat), 1).astype(F32)
    choose = []
    for index in range(ROUNDS):
        blocks = []
        for replica in range(groups):
            wanted = tiles[replica, 2 + index : 3 + index, 0:1] * float(rows) + inside
            blocks.append(jnp.where(wanted == column, 1.0, 0.0))
        choose.append(jnp.concatenate(blocks, axis=0).astype(BF16))
    finish("gossip", 1, lambda p: owned.at[p], first)

    def through(value):
        return jnp.dot(value, gram, precision=HIGHEST, preferred_element_type=F32)

    state = first[...].reshape(flat, lanes)
    sent = state[:, :rank]
    apart = dot(choose[0], sent.astype(BF16)) - sent
    seen = through(apart)
    spread = [jnp.sum(apart * seen)]
    again = (state[:, rank:] + sent + mixing * seen - through(sent)).astype(BF16)
    sent = again.astype(F32)
    later = dot(choose[1], again) - sent
    spread.append(jnp.sum(later * through(later)))
    answer = jnp.concatenate([mixing * (apart + later), sent], axis=1)
    reply[...] = answer.reshape(groups, rows, lanes)
    cons[g] = jnp.where(row == 0, spread[0], spread[1])
    start("gossip", 2, lambda p: reply.at[p], second)
    start("gossip", 3, lambda p: cons.at[g], cons)
    second[g] = reply[g]
    finish("gossip", 2, lambda p: reply.at[p], second)
    start("mp", 3, lambda p: second, final)
    finish("gossip", 3, lambda p: cons.at[g], cons)
    cons_mp[m] = jnp.sum(cons[...], axis=0)
    start("mp", 4, lambda p: cons_mp.at[m], cons_mp)
    final[m] = second[...]
    finish("mp", 3, lambda p: second, final)
    finish("mp", 4, lambda p: cons_mp.at[m], cons_mp)
    f_ref[...] = final[...]
    drift = jnp.sum(cons_mp[...], axis=0) / total
    stat_ref[0] = norm
    stat_ref[1] = scale
    stat_ref[2] = drift


def blend(scale_ref, w_ref, g_ref, f_ref, p_ref, out_ref, basis):
    rank = p_ref.shape[1]

    @pl.when(pl.program_id(0) == 0)
    def _():
        high, low = high_low(p_ref[...])
        basis[...] = jnp.concatenate([high, high, low], axis=1)

    high, low = high_low(f_ref[:, :rank])
    lead = jnp.concatenate([high, low, high], axis=1)
    term = lax.dot_general(lead, basis[...], (((1,), (1,)), ((), ())), preferred_element_type=F32)
    half = w_ref[0] - scale_ref[0] * g_ref[0, 0].astype(F32) - scale_ref[1] * g_ref[1, 0].astype(F32)
    out_ref[0] = half + term


def body(params, public, gradients, projection, partners):
    groups = lax.axis_size("gossip")
    members = lax.axis_size("mp")
    _, height, columns = params.shape
    rank = projection.shape[1]
    lanes = 2 * rank
    total = groups * height * columns * members
    tile = min(128, height)
    steps = height // tile
    rows = height // (groups * members)

    w_spec = pl.BlockSpec((1, tile, columns), lambda i: (0, i, 0))
    g_spec = pl.BlockSpec((ROUNDS, 1, tile, columns), lambda i: (0, 0, i, 0))
    p_spec = pl.BlockSpec((columns, rank), lambda i: (0, 0))
    row_spec = pl.BlockSpec((tile, lanes), lambda i: (i, 0))
    product = jax.ShapeDtypeStruct((height, lanes), F32)
    a, b, d, gram, squares = pl.pallas_call(
        functools.partial(project, members),
        grid=(steps,),
        in_specs=[w_spec, g_spec, pl.BlockSpec((1, tile, rank), lambda i: (0, i, 0)), p_spec],
        out_specs=[row_spec, row_spec, row_spec,
                   pl.BlockSpec((rank, lanes), lambda i: (0, 0)),
                   pl.BlockSpec((ROUNDS, 8, columns), lambda i: (0, 0, 0))],
        out_shape=[product, product, product,
                   jax.ShapeDtypeStruct((rank, lanes), F32),
                   jax.ShapeDtypeStruct((ROUNDS, 8, columns), F32)],
        scratch_shapes=[pltpu.VMEM((columns, lanes), BF16), pltpu.VMEM((rank, lanes), F32)],
        compiler_params=pltpu.CompilerParams(dimension_semantics=("arbitrary",)),
        name="project",
    )(params, gradients, public, projection)

    split = (members, groups, rows, lanes)
    pieces = (groups, rows, lanes)
    final, stats = pl.pallas_call(
        functools.partial(exchange, groups, members, total),
        in_specs=[VMEM] * 5 + [SMEM],
        out_specs=[VMEM, VMEM],
        out_shape=[jax.ShapeDtypeStruct(split, F32), jax.ShapeDtypeStruct((3, 8, 128), F32)],
        scratch_shapes=[
            pltpu.VMEM((groups, 8, 128), F32),
            pltpu.VMEM((members, 8, 128), F32),
            pltpu.VMEM((members, rank, lanes), F32),
            pltpu.VMEM(split, F32),
            pltpu.VMEM(split, F32),
            pltpu.VMEM(pieces, F32),
            pltpu.VMEM(pieces, F32),
            pltpu.VMEM(pieces, F32),
            pltpu.VMEM(pieces, F32),
            pltpu.VMEM(split, F32),
            pltpu.VMEM((groups, 8, 128), F32),
            pltpu.VMEM((members, 8, 128), F32),
            pltpu.SemaphoreType.DMA((4, groups)),
            pltpu.SemaphoreType.DMA((4, groups)),
            pltpu.SemaphoreType.DMA((5, members)),
            pltpu.SemaphoreType.DMA((5, members)),
        ],
        compiler_params=pltpu.CompilerParams(collective_id=0, has_side_effects=True),
        name="exchange",
    )(a.reshape(split), b.reshape(split), d.reshape(split), gram, squares, partners)

    final = final.reshape(height, lanes)
    weights = pl.pallas_call(
        blend,
        grid=(steps,),
        in_specs=[SMEM, w_spec, g_spec, row_spec, p_spec],
        out_specs=w_spec,
        out_shape=jax.ShapeDtypeStruct(params.shape, F32),
        scratch_shapes=[pltpu.VMEM((columns, 3 * rank), BF16)],
        compiler_params=pltpu.CompilerParams(dimension_semantics=("arbitrary",)),
        name="blend",
    )(stats[1, :ROUNDS, 0], params, gradients, final, projection)
    return (weights, final[None, :, rank:], stats[2, :ROUNDS, 0], stats[0, :ROUNDS, 0])


def solution(mesh):
    return jax.shard_map(
        body,
        mesh=mesh,
        in_specs=(
            P("gossip", None, "mp"),
            P("gossip", None, None),
            P(None, "gossip", None, "mp"),
            P("mp", None),
            P(None, "gossip"),
        ),
        out_specs=(P("gossip", None, "mp"), P("gossip", None, None), P(), P()),
        check_vma=False,
    )
```

time: 275 us -> 79.2 us (0.29)
  blocking collectives: 97.9 us -> 0 us
  Pallas kernels: 0 us -> 70.6 us
  matrix products: 64.2 us -> 0 us
  waiting for transfers between devices: 44.8 us -> 0 us
  starting transfers between devices: 25.2 us -> 0 us
  between operations: 17.1 us -> 0.64 us
  other arithmetic: 14.8 us -> 0 us
  local copies, waits for them, and re-layouts: 10.4 us -> 7.42 us
    psum x2 -> x0, blocking collectives: 83.8 us -> none  [the longest x1 42.2 us: body(): drift_list.append(lax.psum(local_drift, ('gossip', 'mp')) / total)]
    pallas_call x0 -> x3, Pallas kernels: none -> 70.6 us  [the longest x1 45.1 us: body(): pl.pallas_call(functools.partial(exchange, groups, members, total), in_sp...]
    dot_general x6 -> x0, matrix products: 64.2 us -> none  [the longest x2 27.6 us: body(): jnp.dot(mate.astype(jnp.float32) - public_state, projection.T, precision=...]
    psum x2 -> x0, waiting for transfers between devices: 31 us -> none  [body(): lax.psum(jnp.dot(half - rebuilt, projection, precision=highest), 'mp')]
    all_to_all x4 -> x0, starting transfers between devices: 25.2 us -> none  [the longest x2 13 us: partner_rows(): lax.all_to_all(reordered, 'gossip', split_axis=0, concat_axis=0, tiled=True)]
    all_gather x1 -> x0, blocking collectives: 14.1 us -> none  [body(): whole_table = lax.all_gather(partners, 'gossip', axis=1, tiled=True)]
    all_to_all x4 -> x0, waiting for transfers between devices: 13.8 us -> none  [the longest x2 9.58 us: partner_rows(): lax.all_to_all(pieces, 'gossip', split_axis=0, concat_axis=0, tiled=True)]
    reduce_sum x1 -> x0, other arithmetic: 5.21 us -> none  [body(): local_squares = jnp.sum(grad_local * grad_local)]
  transfers between devices with their start and end apart: 6 -> 0, of which waited for: 5 -> 0; matrix products, arithmetic and copies ran while one was open for 2% -> 0% of each run, Pallas kernels for 0% -> 0%
where the time goes in v1:
time: 79.2 us; the launch traced here: 78.7 us
  Pallas kernels  70.6 us (89%)
  local copies, waits for them, and re-layouts  7.42 us (9%)
    pallas_call x1, Pallas kernels, body(): pl.pallas_call(functools.partial(exchange, groups, members, total), in_sp...  45.1 us
    pallas_call x1, Pallas kernels, body(): pl.pallas_call(blend, grid=(steps,), in_specs=[SMEM, w_spec, g_spec, row_...  12.8 us
    pallas_call x1, Pallas kernels, body(): pl.pallas_call(functools.partial(project, members), grid=(steps,), in_spe...  12.6 us
    unnamed x8, local copies, waits for them, and re-layouts  5.87 us

profile of v1, /device:TPU:12, one launch (start us, length us, event | category | flops | bytes accessed | tf_op | source)
XLA Modules:
  0.0 78.7 jit_solution(11824732593006269069)
XLA Ops:
  0.6 2.4 %copy.15.p_ref = f32[2048,64]{1,0:T(8,128)} copy(f32[2048,64]{0,1:T(8,128)} %param.8) | data formatting | bytes 1048576 | tf_op args[3]
  3.0 1.9 %copy.14.c_ref = f32[1,1024,64]{2,1,0:T(8,128)} copy(f32[1,1024,64]{1,2,0:T(8,128)} %param.6) | data formatting | bytes 524288 | tf_op args[1]
  5.0 0.0 copy-start.1
  5.0 12.6 %project.1 = (f32[1024,128]{1,0:T(8,128)}, f32[1024,128]{1,0:T(8,128)}, f32[1024,128]{1,0:T(8,128)}, f32[64,128]{1,0:T(8,128)}, f32[2,8,2048]{2,1,0:T(8,128)}) custom-call(f32[1,1024,2048]{2,1,0:T(8,128)} %w_ref.3, bf16[2,1,1024,2048]{3,2,1,0:T(8,128)(2,1)} %g_ref.3, f32[1,1024,64]{2,1,0:T(8,128)} %copy.14.c_ref, f32[2048,64]{1,0:T(8,128)} %copy.15.p_ref), custom_call_target="tpu_custom_call" | custom-call | tf_op jit(solution)/shard_map/project/pallas_call | solution.py:212
  17.6 0.0 copy-done.1
  17.6 0.6 copy.16.partners_ref
  18.2 45.1 %exchange.1 = (f32[2,16,32,128]{3,2,1,0:T(8,128)}, f32[3,8,128]{2,1,0:T(8,128)}) custom-call(f32[2,16,32,128]{3,2,1,0:T(8,128)} %bitcast.8, f32[2,16,32,128]{3,2,1,0:T(8,128)} %bitcast.9, f32[2,16,32,128]{3,2,1,0:T(8,128)} %bitcast.10, f32[64,128]{1,0:T(8,128)} %get-tuple-element.14.gram_ref, f32[2,8,2048]{2,1,0:T(8,128)} %get-tuple-element.15.sq_ref, ...), custom_call_target="tpu_custom_call" | custom-call | tf_op jit(solution)/shard_map/exchange/pallas_call | solution.py:229
  63.4 1.4 %slice_reduce_fusion = (f32[2]{0:T(128)}, f32[2]{0:T(128)}, f32[2]{0:T(128)}) fusion(f32[3,8,128]{2,1,0:T(8,128)} %get-tuple-element.16), kind=kLoop, calls=%fused_computation.1 | loop fusion | bytes 48 | tf_op jit(solution)/shard_map/slice | solution.py:267
  64.8 0.0 copy-start
  64.8 12.8 %blend.1 = f32[1,1024,2048]{2,1,0:T(8,128)} custom-call(f32[2]{0:T(128)} %get-tuple-element.28.scale_ref, f32[1,1024,2048]{2,1,0:T(8,128)} %w_ref.3, bf16[2,1,1024,2048]{3,2,1,0:T(8,128)(2,1)} %g_ref.3, f32[1024,128]{1,0:T(8,128)} %bitcast.6, f32[2048,64]{1,0:T(8,128)} %copy.15.p_ref), custom_call_target="tpu_custom_call" | custom-call | tf_op jit(solution)/shard_map/blend/pallas_call | solution.py:257
  77.6 0.0 copy-done
  77.6 0.2 slice_bitcast_fusion
  77.8 0.9 %copy.18 = f32[1,1024,64]{1,2,0:T(8,128)} copy(f32[1,1024,64]{2,1,0:T(8,128)S(1)} %slice_bitcast_fusion) | data formatting | bytes 524288
Async XLA Ops:
  5.0 12.6 %copy-start.1 = (s32[2,1]{0,1:T(1,128)S(1)}, s32[2,1]{0,1:T(1,128)}, u32[]{:S(2)}) copy-start(s32[2,1]{0,1:T(1,128)} %param.9) | copy-start | bytes 28
  64.8 12.8 %copy-start = (f32[2,16,32,128]{3,2,1,0:T(8,128)S(1)}, f32[2,16,32,128]{3,2,1,0:T(8,128)}, u32[]{:S(2)}) copy-start(f32[2,16,32,128]{3,2,1,0:T(8,128)} %get-tuple-element.17) | copy-start | bytes 1572868

commit v2 on v1

v2 whole, which is shorter than its diff:
```python
import functools

import jax
import jax.numpy as jnp
from jax import lax
from jax.experimental import pallas as pl
from jax.experimental.pallas import tpu as pltpu
from jax.sharding import PartitionSpec as P

ROUNDS = 2
step_size = 1.0
clip_limit = 0.5
mixing = 0.4
epsilon = 1e-06

F32 = jnp.float32
BF16 = jnp.bfloat16
HIGHEST = lax.Precision.HIGHEST
VMEM = pl.BlockSpec(memory_space=pltpu.VMEM)
SMEM = pl.BlockSpec(memory_space=pltpu.SMEM)


def high_low(value):
    high = value.astype(BF16)
    return high, (value - high.astype(F32)).astype(BF16)


def dot(a, b):
    return jnp.dot(a, b, preferred_element_type=F32)


def dot_t(a, b):
    return lax.dot_general(a, b, (((1,), (1,)), ((), ())), preferred_element_type=F32)


def exchange(groups, members, total, w_hbm, g_hbm, c_ref, p_ref, partners_ref, half_hbm, f_ref, stat_ref,
             wv, gv, basis, squares, a_ref, b_ref, d_ref,
             tiles, tiles_mp, grams, local, arrived, owned, first, reply, second, final, cons, cons_mp,
             send_g, recv_g, send_m, recv_m, send_u, recv_u, send_f, recv_f, load_g, load_w, store_w):
    g = lax.axis_index("gossip")
    m = lax.axis_index("mp")
    rows = owned.shape[1]
    lanes = owned.shape[2]
    rank = lanes // 2
    flat = groups * rows
    height, columns = wv.shape
    steps = load_w.shape[0]
    chunk = height // steps

    def span(i):
        return pl.ds(pl.multiple_of(i * chunk, chunk), chunk)

    def each(low, high, act):
        lax.fori_loop(low, high, lambda i, _: (act(i), 0)[1], 0)

    def grad_copy(i):
        return pltpu.make_async_copy(g_hbm.at[:, 0, span(i)], gv.at[:, span(i)], load_g.at[i])

    def weight_copy(i):
        return pltpu.make_async_copy(w_hbm.at[0, span(i)], wv.at[span(i)], load_w.at[i])

    def half_copy(i):
        return pltpu.make_async_copy(wv.at[span(i)], half_hbm.at[0, span(i)], store_w.at[i])

    each(0, steps, lambda i: grad_copy(i).start())
    each(0, steps, lambda i: weight_copy(i).start())

    def peers(count, here, act):
        each(1, count, lambda k: act(lax.rem(here + k, count)))

    barrier = pltpu.get_barrier_semaphore()

    def greet(axis):
        def act(peer):
            pl.semaphore_signal(barrier, inc=1, device_id={axis: peer}, device_id_type=pl.DeviceIdType.MESH)
        return act

    peers(groups, g, greet("gossip"))
    peers(members, m, greet("mp"))

    def copy(axis, slot, src, dst, peer, into):
        send, recv = (send_g, recv_g) if axis == "gossip" else (send_m, recv_m)
        return pltpu.make_async_remote_copy(
            src_ref=src, dst_ref=dst, send_sem=send.at[slot, peer], recv_sem=recv.at[slot, into],
            device_id={axis: peer}, device_id_type=pl.DeviceIdType.MESH)

    def start(axis, slot, source, target):
        count, here = (groups, g) if axis == "gossip" else (members, m)
        peers(count, here, lambda p: copy(axis, slot, source(p), target.at[here], p, here).start())

    def finish(axis, slot, source, target):
        count, here = (groups, g) if axis == "gossip" else (members, m)
        peers(count, here, lambda p: copy(axis, slot, source(p), target.at[p], p, p).wait())

    def part_copy(p, q, into):
        return pltpu.make_async_remote_copy(
            src_ref=local.at[q, p], dst_ref=arrived.at[into, p], send_sem=send_u.at[p, q], recv_sem=recv_u.at[p, into],
            device_id={"mp": q}, device_id_type=pl.DeviceIdType.MESH)

    def result_copy(p, q, into):
        return pltpu.make_async_remote_copy(
            src_ref=second.at[p], dst_ref=final.at[into, p], send_sem=send_f.at[p, q], recv_sem=recv_f.at[p, into],
            device_id={"mp": q}, device_id_type=pl.DeviceIdType.MESH)

    high, low = high_low(p_ref[...])
    basis[...] = jnp.concatenate([high, low], axis=0)
    parts = dot_t(basis[...], basis[...])
    folded = parts + pltpu.roll(parts, rank, 1)
    gram = folded[:rank] + folded[rank:]
    gram_row = lax.broadcasted_iota(jnp.int32, gram.shape, 0)
    gram_col = lax.broadcasted_iota(jnp.int32, gram.shape, 1)
    gram = jnp.where(gram_col < rank, gram, 0.0)
    mixer = jnp.where(gram_row == gram_col, 1.0 / members, 0.0) - gram
    a_ref[...] = lax.dot_general(c_ref[...], mixer, (((0,), (0,)), ((), ())), precision=HIGHEST,
                                 preferred_element_type=F32)
    squares[...] = jnp.zeros_like(squares)
    grams[m] = gram

    def fold(value):
        return value + pltpu.roll(value, rank, 1)

    def grad_step(i):
        grad_copy(i).wait()
        for index in range(ROUNDS):
            grad = gv[index, span(i)]
            wide = grad.astype(F32)
            squares[index] += jnp.sum((wide * wide).reshape(chunk // 8, 8, columns), axis=0)
            product = fold(dot_t(grad, basis[...]))
            if index == 0:
                b_ref[span(i)] = product
            else:
                lane = lax.broadcasted_iota(jnp.int32, product.shape, 1)
                d_ref[span(i)] = jnp.where(lane < rank, 0.0, product)

    def weight_step(i):
        weight_copy(i).wait()
        high, low = high_low(wv[span(i)])
        a_ref[span(i)] += fold(dot_t(high, basis[...]) + dot_t(low, basis[...]))

    each(0, steps, grad_step)
    row = lax.broadcasted_iota(jnp.int32, (8, 128), 0)
    tile = jnp.where(row == 0, jnp.sum(squares[0]), jnp.sum(squares[1]))
    tile = jnp.where(row == 2, partners_ref[0].astype(F32), tile)
    tile = jnp.where(row == 3, partners_ref[1].astype(F32), tile)
    tiles[g] = tile
    pl.semaphore_wait(barrier, groups - 1 + members - 1)

    start("gossip", 0, lambda p: tiles.at[g], tiles)
    start("mp", 0, lambda p: grams.at[m], grams)
    each(0, steps // 2, weight_step)
    finish("gossip", 0, lambda p: tiles.at[g], tiles)
    tiles_mp[m] = jnp.sum(tiles[...], axis=0)
    start("mp", 1, lambda p: tiles_mp.at[m], tiles_mp)
    each(steps // 2, steps, weight_step)
    finish("mp", 1, lambda p: tiles_mp.at[m], tiles_mp)
    norm = jnp.sqrt(jnp.sum(tiles_mp[...], axis=0) / total + epsilon)
    scale = step_size * jnp.minimum(1.0, clip_limit / norm)

    local[...] = (a_ref[...] - scale[0:1, :] * b_ref[...] - scale[1:2, :] * d_ref[...]).reshape(local.shape)
    each(1, groups + 1, lambda k: peers(members, m, lambda q: part_copy(lax.rem(g + k, groups), q, m).start()))
    lane = lax.broadcasted_iota(jnp.int32, (rows, lanes), 1)

    def take(p):
        peers(members, m, lambda q: part_copy(p, q, q).wait_recv())
        summed = local[m, p]
        for index in range(1, members):
            summed = summed + arrived[lax.rem(m + index, members), p]
        return jnp.where(lane < rank, summed.astype(BF16).astype(F32), summed)

    def pass_on(p):
        owned[p] = take(p)
        copy("gossip", 1, owned.at[p], first.at[g], p, g).start()

    peers(groups, g, pass_on)
    first[g] = take(g)

    def half_step(i):
        wide = [gv[index, span(i)].astype(F32) for index in range(ROUNDS)]
        wv[span(i)] = wv[span(i)] - scale[0, 0] * wide[0] - scale[1, 0] * wide[1]
        half_copy(i).start()

    each(0, steps, half_step)

    finish("mp", 0, lambda p: grams.at[m], grams)
    gram = jnp.sum(grams[...], axis=0)[:, :rank]
    inside = lax.broadcasted_iota(jnp.int32, (rows, flat), 0).astype(F32)
    column = lax.broadcasted_iota(jnp.int32, (rows, flat), 1).astype(F32)
    choose = []
    for index in range(ROUNDS):
        blocks = []
        for replica in range(groups):
            wanted = tiles[replica, 2 + index : 3 + index, 0:1] * float(rows) + inside
            blocks.append(jnp.where(wanted == column, 1.0, 0.0))
        choose.append(jnp.concatenate(blocks, axis=0).astype(BF16))
    finish("gossip", 1, lambda p: owned.at[p], first)

    def through(value):
        return jnp.dot(value, gram, precision=HIGHEST, preferred_element_type=F32)

    state = first[...].reshape(flat, lanes)
    sent = state[:, :rank]
    apart = dot(choose[0], sent.astype(BF16)) - sent
    seen = through(apart)
    spread = [jnp.sum(apart * seen)]
    again = (state[:, rank:] + sent + mixing * seen - through(sent)).astype(BF16)
    sent = again.astype(F32)
    later = dot(choose[1], again) - sent
    spread.append(jnp.sum(later * through(later)))
    answer = jnp.concatenate([mixing * (apart + later), sent], axis=1)
    reply[...] = answer.reshape(groups, rows, lanes)
    cons[g] = jnp.where(row == 0, spread[0], spread[1])
    start("gossip", 2, lambda p: reply.at[p], second)
    start("gossip", 3, lambda p: cons.at[g], cons)
    second[g] = reply[g]
    final[m, g] = reply[g]
    peers(members, m, lambda q: result_copy(g, q, m).start())

    def hand_over(p):
        copy("gossip", 2, reply.at[p], second.at[p], p, p).wait()
        final[m, p] = second[p]
        peers(members, m, lambda q: result_copy(p, q, m).start())

    peers(groups, g, hand_over)
    finish("gossip", 3, lambda p: cons.at[g], cons)
    cons_mp[m] = jnp.sum(cons[...], axis=0)
    start("mp", 4, lambda p: cons_mp.at[m], cons_mp)
    each(0, steps, lambda i: half_copy(i).wait())
    each(0, groups, lambda p: peers(members, m, lambda q: part_copy(p, q, q).wait_send()))
    each(0, groups, lambda p: peers(members, m, lambda q: result_copy(p, q, q).wait()))
    finish("mp", 4, lambda p: cons_mp.at[m], cons_mp)
    f_ref[...] = final[...]
    drift = jnp.sum(cons_mp[...], axis=0) / total
    stat_ref[0] = norm
    stat_ref[1] = scale
    stat_ref[2] = drift


def blend(h_ref, f_ref, p_ref, stat_ref, out_ref, c_ref, drift_ref, norm_ref, basis):
    rank = p_ref.shape[0]

    @pl.when(pl.program_id(0) == 0)
    def _():
        high, low = high_low(p_ref[...])
        basis[...] = jnp.concatenate([high, high, low], axis=0)
        for index in range(ROUNDS):
            norm_ref[index] = jnp.max(stat_ref[0, index : index + 1, :])
            drift_ref[index] = jnp.max(stat_ref[2, index : index + 1, :])

    high, low = high_low(f_ref[:, :rank])
    out_ref[0] = h_ref[0] + dot(jnp.concatenate([high, low, high], axis=1), basis[...])
    c_ref[...] = f_ref[...].T[rank:]


def body(params, public, gradients, projection, partners):
    groups = lax.axis_size("gossip")
    members = lax.axis_size("mp")
    _, height, columns = params.shape
    rank = projection.shape[1]
    lanes = 2 * rank
    total = groups * height * columns * members
    tile = min(128, height)
    steps = height // tile
    rows = height // (groups * members)
    split = (members, groups, rows, lanes)
    pieces = (groups, rows, lanes)
    basis = projection.T
    anywhere = pl.BlockSpec(memory_space=pl.ANY)
    dma = pltpu.SemaphoreType.DMA
    half, final, stats = pl.pallas_call(
        functools.partial(exchange, groups, members, total),
        in_specs=[anywhere, anywhere, VMEM, VMEM, SMEM],
        out_specs=[anywhere, VMEM, VMEM],
        out_shape=[jax.ShapeDtypeStruct(params.shape, F32), jax.ShapeDtypeStruct(split, F32),
                   jax.ShapeDtypeStruct((3, 8, 128), F32)],
        scratch_shapes=[
            pltpu.VMEM((height, columns), F32),
            pltpu.VMEM((ROUNDS, height, columns), BF16),
            pltpu.VMEM((lanes, columns), BF16),
            pltpu.VMEM((ROUNDS, 8, columns), F32),
            pltpu.VMEM((height, lanes), F32),
            pltpu.VMEM((height, lanes), F32),
            pltpu.VMEM((height, lanes), F32),
            pltpu.VMEM((groups, 8, 128), F32),
            pltpu.VMEM((members, 8, 128), F32),
            pltpu.VMEM((members, rank, lanes), F32),
            pltpu.VMEM(split, F32),
            pltpu.VMEM(split, F32),
            pltpu.VMEM(pieces, F32),
            pltpu.VMEM(pieces, F32),
            pltpu.VMEM(pieces, F32),
            pltpu.VMEM(pieces, F32),
            pltpu.VMEM(split, F32),
            pltpu.VMEM((groups, 8, 128), F32),
            pltpu.VMEM((members, 8, 128), F32),
            dma((4, groups)), dma((4, groups)), dma((5, members)), dma((5, members)),
            dma((groups, members)), dma((groups, members)), dma((groups, members)), dma((groups, members)),
            dma((steps,)), dma((steps,)), dma((steps,)),
        ],
        compiler_params=pltpu.CompilerParams(collective_id=0, has_side_effects=True),
        name="exchange",
    )(params, gradients, public[0].T, basis, partners.reshape(ROUNDS))

    w_spec = pl.BlockSpec((1, tile, columns), lambda i: (0, i, 0))
    weights, coefs, drift, norm = pl.pallas_call(
        blend,
        grid=(steps,),
        in_specs=[w_spec, pl.BlockSpec((tile, lanes), lambda i: (i, 0)),
                  pl.BlockSpec((rank, columns), lambda i: (0, 0)), VMEM],
        out_specs=[w_spec, pl.BlockSpec((rank, tile), lambda i: (0, i)), SMEM, SMEM],
        out_shape=[jax.ShapeDtypeStruct(params.shape, F32), jax.ShapeDtypeStruct((rank, height), F32),
                   jax.ShapeDtypeStruct((ROUNDS,), F32), jax.ShapeDtypeStruct((ROUNDS,), F32)],
        scratch_shapes=[pltpu.VMEM((3 * rank, columns), BF16)],
        compiler_params=pltpu.CompilerParams(dimension_semantics=("arbitrary",)),
        name="blend",
    )(half, final.reshape(height, lanes), basis, stats)
    return (weights, coefs.T[None], drift, norm)


def solution(mesh):
    return jax.shard_map(
        body,
        mesh=mesh,
        in_specs=(
            P("gossip", None, "mp"),
            P("gossip", None, None),
            P(None, "gossip", None, "mp"),
            P("mp", None),
            P(None, "gossip"),
        ),
        out_specs=(P("gossip", None, "mp"), P("gossip", None, None), P(), P()),
        check_vma=False,
    )
```

time: 79.2 us -> 57.7 us (0.73)
  Pallas kernels: 70.6 us -> 56 us
  local copies, waits for them, and re-layouts: 7.42 us -> 0 us
    pallas_call x2 -> x1, Pallas kernels: 25.5 us -> 10.4 us  [body(): pl.pallas_call(blend, grid=(steps,), in_specs=[w_spec, pl.BlockSpec((tile...]
    unnamed x8 -> x0, local copies, waits for them, and re-layouts: 5.87 us -> none
    slice x1 -> x0, local copies, waits for them, and re-layouts: 1.36 us -> none  [body(): stats[0, :ROUNDS, 0]]
where the time goes in v2:
time: 57.7 us; the launch traced here: 56.6 us
  Pallas kernels  56 us (97%)
  between operations  0.64 us (1%)
    pallas_call x1, Pallas kernels, body(): pl.pallas_call(functools.partial(exchange, groups, members, total), in_sp...  45.6 us
    pallas_call x1, Pallas kernels, body(): pl.pallas_call(blend, grid=(steps,), in_specs=[w_spec, pl.BlockSpec((tile...  10.4 us

profile of v2, /device:TPU:12, one launch (start us, length us, event | category | flops | bytes accessed | tf_op | source)
XLA Modules:
  0.0 56.6 jit_solution(3483169803987036083)
XLA Ops:
  0.6 45.6 %exchange.1 = (f32[1,1024,2048]{2,1,0:T(8,128)}, f32[2,16,32,128]{3,2,1,0:T(8,128)}, f32[3,8,128]{2,1,0:T(8,128)}) custom-call(f32[1,1024,2048]{2,1,0:T(8,128)} %w_hbm.1, bf16[2,1,1024,2048]{3,2,1,0:T(8,128)(2,1)} %g_hbm.1, f32[64,1024]{1,0:T(8,128)} %bitcast.12, f32[64,2048]{1,0:T(8,128)} %bitcast.9, s32[2]{0:T(128)} %bitcast.13), custom_call_target="tpu_custom_call" | custom-call | tf_op jit(solution)/shard_map/exchange/pallas_call | solution.py:269
  46.3 10.4 %blend.1 = (f32[1,1024,2048]{2,1,0:T(8,128)}, f32[64,1024]{1,0:T(8,128)}, f32[2]{0:T(128)}, f32[2]{0:T(128)}) custom-call(f32[1,1024,2048]{2,1,0:T(8,128)} %get-tuple-element.11.h_ref, f32[1024,128]{1,0:T(8,128)} %bitcast.11, f32[64,2048]{1,0:T(8,128)} %bitcast.10, f32[3,8,128]{2,1,0:T(8,128)} %get-tuple-element.13.stat_ref), custom_call_target="tpu_custom_call" | custom-call | tf_op jit(solution)/shard_map/blend/pallas_call | solution.py:304
